TPU v7x, 32 devices: a whole 2x2x4 slice. The times are simulated.
32 devices in a mesh: date: 16 (over z, y, x), prod: 2 (over core).
Axes of the slice: x: 2, y: 2, z: 4, core: 2. Of those that a mesh axis runs over, the one named last changes fastest.
Arguments:
- daily_sales: float32 [256, 512, 128], P('prod', 'date'), may hold values from -2.5 to 2.5
- week_id: int32 [512], P('date'), may hold values from 0 to 102, never falling along the last dimension, each value on 1 to 7 neighbouring positions
- month_id: int32 [512], P('date'), may hold values from 0 to 21, never falling along the last dimension, each value on 1 to 31 neighbouring positions
- year_id: int32 [512], P('date'), may hold values from 0 to 1, never falling along the last dimension, each value on 1 to 366 neighbouring positions
Outputs:
- running: float32 [256, 512, 128], P('prod', 'date')
- week_total: float32 [256, 512, 128], P('prod', 'date')
- month_total: float32 [256, 512, 128], P('prod', 'date')
- year_total: float32 [256, 512, 128], P('prod', 'date')
- store_rollup: float32 [4, 512, 128], P(None, 'date')
Inputs may be any that keep to these rules, and one draw needn't show every extreme that they name: `week_id`: starts at 0 and never falls along the dates; each week covers 1 to 7 consecutive dates and some cover exactly 7. `month_id`: starts at 0 and never falls along the dates; each month covers 1 to 31 consecutive dates and some cover exactly 31; months need not line up with weeks. `year_id`: starts at 0 and never falls along the dates; each year covers 1 to 366 consecutive dates and some cover exactly 366; years need not line up with weeks or months.
All inputs are finite; a program needn't handle non-finite values.
Results may differ from a plain program's by a relative error of at most 0.000094.
Values sent between devices are 32-bit elements.
A program may use at most 64 MiB of HBM per device.

v0:
```python
import jax
import jax.numpy as jnp
from jax import lax
from jax.sharding import PartitionSpec as P

far_index = 1 << 30


def from_behind(block, axis, distance):
    devices = range(lax.axis_size(axis))
    route = [(i - distance, i) for i in devices if i - distance in devices]
    return lax.ppermute(block, axis, route)


def carried_in(value, axis, join, neutral, backward):
    count, mine = (lax.axis_size(axis), lax.axis_index(axis))
    pieces = jax.tree.map(lambda part: lax.all_gather(part, axis), value)
    if backward:
        pieces = jax.tree.map(lambda part: part[::-1], pieces)
        mine = count - 1 - mine
    running = jax.tree.map(
        lambda part, zero: jnp.full_like(part, 0) + jnp.asarray(zero, part.dtype), value, neutral
    )

    def step(position, running):
        longer = join(running, jax.tree.map(lambda part: part[position], pieces))
        return jax.tree.map(lambda new, old: jnp.where(position < mine, new, old), longer, running)

    return lax.fori_loop(0, count - 1, step, running)


def forward(earlier, latter):
    top_early, sums_early = earlier
    top_later, sums_later = latter
    inside = (top_later <= top_early)[:, None, None]
    return (jnp.maximum(top_early, top_later), sums_later + jnp.where(inside, sums_early, 0.0))


def backward(earlier, latter):
    low_early, sums_early = earlier
    low_later, sums_later = latter
    inside = (low_later >= low_early)[:, None, None]
    return (jnp.minimum(low_early, low_later), sums_later + jnp.where(inside, sums_early, 0.0))


def match_keep(ids_seen, ids_own, partial_value):
    return jnp.where((ids_seen == ids_own)[:, None, None], partial_value, 0.0)


def local(daily_sales, week_id, month_id, year_id):
    columns = daily_sales.shape[0]
    span_len = daily_sales.shape[1]
    level_ids = jnp.stack([jnp.zeros_like(week_id), week_id, month_id, year_id])
    offsets = lax.iota(jnp.int32, span_len)
    lower = (offsets[None, :] <= offsets[:, None]).astype(jnp.float32)
    matches = (level_ids[1:, :, None] == level_ids[1:, None, :]).astype(jnp.float32)
    mixers = jnp.concatenate([lower[None], matches], axis=0)
    within = jnp.einsum("kij,pjs->kpis", mixers, daily_sales, precision=lax.Precision.HIGHEST)
    tail_sums = within[:, :, -1, :]
    head_sums = within[1:, :, 0, :]
    first_ids = level_ids[:, 0]
    last_ids = level_ids[:, -1]
    left_ids, left_sums = from_behind((last_ids[1:3], tail_sums[1:3]), "date", 1)
    right_ids, right_sums = from_behind((first_ids[1:3], head_sums[0:2]), "date", -1)
    outer_ids = jnp.stack([last_ids[0], last_ids[3]])
    outer_sums = jnp.stack([tail_sums[0], tail_sums[3]])
    start = (jnp.full((2,), -1, jnp.int32), jnp.zeros_like(outer_sums))
    top_prev, sums_prev = carried_in((outer_ids, outer_sums), "date", forward, start, False)
    outer_in = match_keep(top_prev, jnp.stack([first_ids[0], first_ids[3]]), sums_prev)
    finish = (jnp.full((1,), far_index, jnp.int32), jnp.zeros_like(head_sums[2:]))
    low_next, sums_next = carried_in((first_ids[3:], head_sums[2:]), "date", backward, finish, True)
    middle_in = match_keep(left_ids, first_ids[1:3], left_sums)
    carry_in = jnp.concatenate([outer_in[:1], middle_in, outer_in[1:]], axis=0)
    middle_back = match_keep(right_ids, last_ids[1:3], right_sums)
    carry_back = jnp.concatenate(
        [middle_back, match_keep(low_next, last_ids[3:], sums_next)], axis=0
    )
    start_gain = (level_ids[1:] == first_ids[1:, None]).astype(jnp.float32)
    end_gain = (level_ids[1:] == last_ids[1:, None]).astype(jnp.float32)
    running = within[0] + carry_in[0][:, None, :]
    levels = (
        within[1:]
        + carry_in[1:, :, None, :] * start_gain[:, None, :, None]
        + carry_back[:, :, None, :] * end_gain[:, None, :, None]
    )
    product_terms = jnp.concatenate(
        [jnp.sum(running, axis=0)[None], jnp.sum(levels, axis=1)], axis=0
    )
    store_rollup = lax.psum(product_terms, "prod")
    return (running, levels[0, :columns], levels[1, :columns], levels[2, :columns], store_rollup)


def solution(mesh):
    return jax.shard_map(
        local,
        mesh=mesh,
        in_specs=(P("prod", "date", None), P("date"), P("date"), P("date")),
        out_specs=(
            P("prod", "date", None),
            P("prod", "date", None),
            P("prod", "date", None),
            P("prod", "date", None),
            P(None, "date", None),
        ),
        check_vma=False,
    )
```

profile of v0, /device:TPU:0, one launch (start us, length us, event | category | flops | bytes accessed | tf_op | source)
XLA Modules:
  0.0 187.9 jit_solution(4630445050261132228)
XLA Ops:
  8.9 3.4 %convolution_bitcast_fusion = f32[4,128,32,128]{3,2,1,0:T(8,128)S(1)} fusion(f32[128,32,128]{2,1,0:T(8,128)S(1)} %copy-done, pred[3,32,32]{2,1,0:T(32,128)(4,1)S(1)} %broadcast_compare_fusion, pred[1,32,32]{2,1,0:T(32,128)(4,1)S(1)} %iota_compare_fusion), kind=kOutput, calls=%fused_computation.11 | convolution fusion | flops 805310464 | bytes 10489856 | tf_op jit(solution)/shard_map/kij,pjs->kpis/dot_general | solution.py:58
  12.3 3.2 %copy-done.1 = f32[4,128,32,128]{3,2,1,0:T(8,128)} copy-done((f32[4,128,32,128]{3,2,1,0:T(8,128)}, f32[4,128,32,128]{3,2,1,0:T(8,128)S(1)}, u32[]{:S(2)}) %copy-start.1) | copy-done | bytes 8388632
  16.6 4.9 %collective-permute-start = (s32[2]{0:T(128)S(1)}, s32[2]{0:T(128)S(1)}, u32[]{:S(2)}, u32[]{:S(2)}) collective-permute-start(s32[2]{0:T(128)S(1)} %get-tuple-element.291), channel_id=1, source_target_pairs={{0,2},{2,4},{4,6},{6,8},{8,10},{10,12},{12,14},{14,16},{16,18},{18... | collective-permute-start | bytes 32 | tf_op jit(solution)/shard_map/ppermute | solution.py:12
  21.5 1.7 fusion.12
  23.2 3.4 %collective-permute-start.1 = (f32[2,128,128]{2,1,0:T(8,128)S(1)}, f32[2,128,128]{2,1,0:T(8,128)S(1)}, u32[]{:S(2)}, u32[]{:S(2)}) collective-permute-start(f32[2,128,128]{2,1,0:T(8,128)S(1)} %bitcast.81), channel_id=1, source_target_pairs={{0,2},{2,4},{4,6},{6,8},{8,10},{10,12},{12,14},{14,16},{16,18},{18... | collective-permute-start | bytes 393224 | tf_op jit(solution)/shard_map/ppermute | solution.py:12
  26.6 1.3 collective-permute-start.2
  27.9 1.3 collective-permute-start.3
  32.8 1.4 bitcast_dynamic-update-slice_fusion
  34.1 17.9 %all-reduce.3 = (s32[32]{0:T(128)S(1)}, s32[16]{0:T(128)S(1)}) all-reduce(s32[32]{0:T(128)S(1)} %pad_dynamic-update-slice_fusion, s32[16]{0:T(128)S(1)} %bitcast_dynamic-update-slice_fusion), channel_id=2, replica_groups=mesh['date'=16,'prod'=2] {'date'}, use_global_device_ids=true, to_apply=%add.1 | all-reduce | flops 48 | bytes 384
  53.2 21.4 %all-gather.8.cloned.1.call-done = f32[16,128,1,128]{3,1,2,0:T(8,128)} async-done(((f32[1,128,1,128]{3,1,2,0:T(8,128)}), f32[16,128,1,128]{3,1,2,0:T(8,128)}) %all-gather.8.cloned.1.call-update) | async-done | bytes 1048592 | tf_op jit(solution)/shard_map/all_gather | solution.py:17
  74.6 1.3 reverse_bitcast_fusion
  75.9 28.3 %while.33 = (s32[]{:T(128)}, s32[1]{0:T(128)}, f32[1,128,128]{2,1,0:T(8,128)S(1)}, s32[]{:T(128)}, s32[16,1]{0,1:T(1,128)S(1)}, /*index=5*/f32[16,1,128,128]{3,2,1,0:T(8,128)S(1)}, s32[]{:T(128)}, s32[]{:T(128)}) while((s32[]{:T(128)}, s32[1]{0:T(128)}, f32[1,128,128]{2,1,0:T(8,128)S(1)}, s32[]{:T(128)}, s32[16,1]{0,1:T(1,128)S(1)}, ...), condition=%wide.region_3.4_spmd.clone, body=%wide.region_2.3_spmd.clone.sunk | while | flops 65543 | bytes 196764 | solution.py:29
  105.7 31.5 %all-gather.6.cloned.1.call-done = f32[32,128,128]{2,1,0:T(8,128)} async-done(((f32[2,128,128]{2,1,0:T(8,128)}), f32[32,128,128]{2,1,0:T(8,128)}) %all-gather.6.cloned.1.call-update) | async-done | bytes 2097168 | tf_op jit(solution)/shard_map/all_gather | solution.py:17
  137.3 15.9 %while.32 = (s32[]{:T(128)}, s32[2]{0:T(128)S(1)}, f32[2,128,128]{2,1,0:T(8,128)S(1)}, s32[]{:T(128)}, s32[16,2]{1,0:T(8,128)S(1)}, /*index=5*/f32[16,2,128,128]{3,2,1,0:T(8,128)}, s32[]{:T(128)}, s32[]{:T(128)}) while((s32[]{:T(128)}, s32[2]{0:T(128)S(1)}, f32[2,128,128]{2,1,0:T(8,128)S(1)}, s32[]{:T(128)}, ...), condition=%wide.region_1.2_spmd.clone, body=%wide.region_0.1_spmd.clone.sunk | while | flops 131086 | bytes 393380 | solution.py:29
  137.3 1.0 fusion.18
  138.4 1.0 fusion.18
  139.4 1.0 fusion.18
  140.5 1.0 fusion.18
  151.1 1.0 fusion.18
  154.1 3.2 %fusion.8 = (f32[32,128]{1,0:T(8,128)S(1)}, f32[128,32,128]{2,1,0:T(8,128)}) fusion(f32[128,128]{1,0:T(8,128)S(1)} %get-tuple-element.332, f32[4,128,32,128]{3,2,1,0:T(8,128)} %copy-done.1), kind=kLoop, calls=%fused_computation.45 | loop fusion | flops 1044480 | bytes 4276224 | tf_op jit(solution)/shard_map/reduce_sum | solution.py:87
  157.3 5.3 %fusion.10 = (f32[3,32,128]{2,1,0:T(8,128)S(1)}, f32[3,128,32,128]{3,2,1,0:T(8,128)}) fusion(f32[3,32]{1,0:T(4,128)S(1)} %get-tuple-element.334, f32[3,128,128]{2,1,0:T(8,128)S(1)} %pad_maximum_fusion.1, f32[3,32]{1,0:T(4,128)S(1)} %get-tuple-element.333, f32[3,128,128]{2,1,0:T(8,128)S(1)} %pad_maximum_fusion, f32[4,128,32,128]{3,2,1,0:T(8,128)} %copy-done.1), kind=kLoop, calls=%fused_computation.46 | loop fusion | flops 7852032 | bytes 13026048 | tf_op jit(solution)/shard_map/reduce_sum | solution.py:87
  163.2 5.7 %slice_bitcast_fusion = (f32[128,32,128]{2,1,0:T(8,128)}, f32[128,32,128]{2,1,0:T(8,128)}, f32[128,32,128]{2,1,0:T(8,128)}) fusion(f32[3,128,32,128]{3,2,1,0:T(8,128)} %get-tuple-element.322), kind=kLoop, calls=%fused_computation.12 | loop fusion | bytes 12582912 | tf_op jit(solution)/shard_map/squeeze | solution.py:90
  168.9 10.9 %all-reduce.6.cloned.1.call-done = f32[4,32,128]{2,1,0:T(8,128)} async-done(((f32[4,32,128]{2,1,0:T(8,128)}), f32[4,32,128]{2,1,0:T(8,128)}) %all-reduce.6.cloned.1.call-update) | async-done | bytes 65552 | tf_op jit(solution)/shard_map/psum | solution.py:89
  179.9 1.5 copy.49
  (121 shorter events, 28.6 us)
Async XLA Ops:
  7.2 1.7 copy-start
  7.2 23.6 %copy-start.5 = (u32[32]{0:T(128)S(1)}, u32[32]{0:T(128)}, u32[]{:S(2)}) copy-start(u32[32]{0:T(128)} %constant.81) | copy-start | bytes 388
  7.2 9.2 %copy-start.4 = (s32[32]{0:T(128)S(1)}, s32[32]{0:T(128)}, u32[]{:S(2)}) copy-start(s32[32]{0:T(128)} %param.9) | copy-start | bytes 388
  7.2 9.2 %copy-start.3 = (s32[32]{0:T(128)S(1)}, s32[32]{0:T(128)}, u32[]{:S(2)}) copy-start(s32[32]{0:T(128)} %param.10) | copy-start | bytes 388
  7.2 22.8 %copy-start.2 = (s32[32]{0:T(128)S(1)}, s32[32]{0:T(128)}, u32[]{:S(2)}) copy-start(s32[32]{0:T(128)} %param.11) | copy-start | bytes 388
  7.2 67.4 %all-gather.8.cloned.1.call-start = ((), (), s32[]{:S(2)}) async-start(), calls=%async_computation.2 | async-start | bytes 1114112 | tf_op jit(solution)/shard_map/all_gather | solution.py:17
  12.3 3.2 %copy-start.1 = (f32[4,128,32,128]{3,2,1,0:T(8,128)}, f32[4,128,32,128]{3,2,1,0:T(8,128)S(1)}, u32[]{:S(2)}) copy-start(f32[4,128,32,128]{3,2,1,0:T(8,128)S(1)} %convolution_bitcast_fusion) | copy-start | bytes 25165828
  16.3 120.9 %all-gather.6.cloned.1.call-start = ((), (), s32[]{:S(2)}) async-start(), calls=%async_computation.1 | async-start | bytes 2228224 | tf_op jit(solution)/shard_map/all_gather | solution.py:17
  16.6 35.7 %collective-permute-start = (s32[2]{0:T(128)S(1)}, s32[2]{0:T(128)S(1)}, u32[]{:S(2)}, u32[]{:S(2)}) collective-permute-start(s32[2]{0:T(128)S(1)} %get-tuple-element.291), channel_id=1, source_target_pairs={{0,2},{2,4},{4,6},{6,8},{8,10},{10,12},{12,14},{14,16},{16,18},{18... | collective-permute-start | bytes 32 | tf_op jit(solution)/shard_map/ppermute | solution.py:12
  23.2 29.2 %collective-permute-start.1 = (f32[2,128,128]{2,1,0:T(8,128)S(1)}, f32[2,128,128]{2,1,0:T(8,128)S(1)}, u32[]{:S(2)}, u32[]{:S(2)}) collective-permute-start(f32[2,128,128]{2,1,0:T(8,128)S(1)} %bitcast.81), channel_id=1, source_target_pairs={{0,2},{2,4},{4,6},{6,8},{8,10},{10,12},{12,14},{14,16},{16,18},{18... | collective-permute-start | bytes 393224 | tf_op jit(solution)/shard_map/ppermute | solution.py:12
  26.6 25.7 %collective-permute-start.2 = (s32[2]{0:T(128)S(1)}, s32[2]{0:T(128)S(1)}, u32[]{:S(2)}, u32[]{:S(2)}) collective-permute-start(s32[2]{0:T(128)S(1)} %get-tuple-element.292), channel_id=1, source_target_pairs={{2,0},{4,2},{6,4},{8,6},{10,8},{12,10},{14,12},{16,14},{18,16},{20... | collective-permute-start | bytes 32 | tf_op jit(solution)/shard_map/ppermute | solution.py:12
  27.9 24.5 %collective-permute-start.3 = (f32[2,128,128]{2,1,0:T(8,128)S(1)}, f32[2,128,128]{2,1,0:T(8,128)S(1)}, u32[]{:S(2)}, u32[]{:S(2)}) collective-permute-start(f32[2,128,128]{2,1,0:T(8,128)S(1)} %bitcast.80), channel_id=1, source_target_pairs={{2,0},{4,2},{6,4},{8,6},{10,8},{12,10},{14,12},{16,14},{18,16},{20... | collective-permute-start | bytes 393224 | tf_op jit(solution)/shard_map/ppermute | solution.py:12
  29.9 149.9 %all-reduce.6.cloned.1.call-start = ((), (), s32[]{:S(2)}) async-start(), calls=%async_computation | async-start | bytes 131072 | tf_op jit(solution)/shard_map/psum | solution.py:89
Sparse Core Ops, SparseCore 0:
  16.5 58.0 all-gather.7
  77.9 59.2 all-gather.5
  163.3 16.4 all-reduce.5
where the time goes:
time: 189 us; the launch traced here: 188 us
  waiting for transfers between devices  63.9 us (34%)
  other arithmetic  29.1 us (15%)
  local copies, waits for them, and re-layouts  27.6 us (15%)
  loops' own time  19.6 us (10%)
  blocking collectives  17.9 us (9%)
  between operations  15.2 us (8%)
  starting transfers between devices  11 us (6%)
  matrix products  3.44 us (2%)
    all_gather x2, waiting for transfers between devices, carried_in(): pieces = jax.tree.map(lambda part: lax.all_gather(part, axis), value)  52.9 us
    another operation x2, loops' own time, carried_in(): return lax.fori_loop(0, count - 1, step, running)  19.6 us
    unnamed x1, blocking collectives  17.9 us
    select_n x45, other arithmetic, step(): jnp.where(position < mine, new, old)  15.5 us
    psum x1, waiting for transfers between devices, local(): store_rollup = lax.psum(product_terms, 'prod')  10.9 us
    ppermute x4, starting transfers between devices, from_behind(): return lax.ppermute(block, axis, route)  10.9 us
    unnamed x20, local copies, waits for them, and re-layouts  9.45 us
    dynamic_slice x15, local copies, waits for them, and re-layouts, step(): longer = join(running, jax.tree.map(lambda part: part[position], pieces))  8.89 us
  transfers between devices with their start and end apart: 7, of which 3 were waited for; matrix products, arithmetic and copies ran while one was open for 13% of the time, Pallas kernels for 0%

commit v1 on v0

--- a/solution.py
+++ b/solution.py
@@ -86,7 +86,12 @@
     product_terms = jnp.concatenate(
         [jnp.sum(running, axis=0)[None], jnp.sum(levels, axis=1)], axis=0
     )
-    store_rollup = lax.psum(product_terms, "prod")
+
+    def shifts_all_bring(payload, shard_axis):
+        block_now = lax.all_gather(payload, axis_name=shard_axis)
+        return jnp.sum(block_now, axis=0)
+
+    store_rollup = shifts_all_bring(product_terms, "prod")
     return (running, levels[0, :columns], levels[1, :columns], levels[2, :columns], store_rollup)
 
 

time: 189 us -> 174 us (0.921)
  waiting for transfers between devices: 63.9 us -> 52.9 us
  local copies, waits for them, and re-layouts: 27.6 us -> 23.2 us
  blocking collectives: 17.9 us -> 19.8 us
    psum x1 -> x0, waiting for transfers between devices: 10.9 us -> none  [local(): store_rollup = lax.psum(product_terms, 'prod')]
    squeeze x1, local copies, waits for them, and re-layouts: 5.73 us -> 2.87 us  [local(): levels[2, :columns]]
    all_gather x0 -> x1, blocking collectives: none -> 1.9 us  [shifts_all_bring(): block_now = lax.all_gather(payload, axis_name=shard_axis)]
    unnamed x20 -> x19, local copies, waits for them, and re-layouts: 9.45 us -> 7.93 us
  transfers between devices with their start and end apart: 7 -> 6, of which waited for: 3 -> 2; matrix products, arithmetic and copies ran while one was open for 13% -> 11% of each run, Pallas kernels for 0% -> 0%
where the time goes in v1:
time: 174 us; the launch traced here: 173 us
  waiting for transfers between devices  52.9 us (30%)
  other arithmetic  27.3 us (16%)
  local copies, waits for them, and re-layouts  23.2 us (13%)
  blocking collectives  19.8 us (11%)
  loops' own time  19.6 us (11%)
  between operations  15.6 us (9%)
  starting transfers between devices  10.9 us (6%)
  matrix products  3.44 us (2%)
    all_gather x2, waiting for transfers between devices, carried_in(): pieces = jax.tree.map(lambda part: lax.all_gather(part, axis), value)  52.9 us
    another operation x2, loops' own time, carried_in(): return lax.fori_loop(0, count - 1, step, running)  19.6 us
    unnamed x1, blocking collectives  17.9 us
    select_n x45, other arithmetic, step(): jnp.where(position < mine, new, old)  15.5 us
    ppermute x4, starting transfers between devices, from_behind(): return lax.ppermute(block, axis, route)  10.9 us
    dynamic_slice x15, local copies, waits for them, and re-layouts, step(): longer = join(running, jax.tree.map(lambda part: part[position], pieces))  8.86 us
    unnamed x19, local copies, waits for them, and re-layouts  7.93 us
    reduce_sum x1, other arithmetic, local(): jnp.sum(levels, axis=1)  3.58 us
  transfers between devices with their start and end apart: 6, of which 2 were waited for; matrix products, arithmetic and copies ran while one was open for 11% of the time, Pallas kernels for 0%

profile of v1, /device:TPU:0, one launch (start us, length us, event | category | flops | bytes accessed | tf_op | source)
XLA Modules:
  0.0 172.9 jit_solution(8238879962772422104)
XLA Ops:
  8.9 3.4 %convolution_bitcast_fusion = f32[4,128,32,128]{3,2,1,0:T(8,128)S(1)} fusion(f32[128,32,128]{2,1,0:T(8,128)S(1)} %copy-done, pred[3,32,32]{2,1,0:T(32,128)(4,1)S(1)} %broadcast_compare_fusion, pred[1,32,32]{2,1,0:T(32,128)(4,1)S(1)} %iota_compare_fusion), kind=kOutput, calls=%fused_computation.11 | convolution fusion | flops 805310464 | bytes 10489856 | tf_op jit(solution)/shard_map/kij,pjs->kpis/dot_general | solution.py:58
  12.3 3.2 %copy-done.1 = f32[4,128,32,128]{3,2,1,0:T(8,128)} copy-done((f32[4,128,32,128]{3,2,1,0:T(8,128)}, f32[4,128,32,128]{3,2,1,0:T(8,128)S(1)}, u32[]{:S(2)}) %copy-start.1) | copy-done | bytes 8388632
  16.6 4.9 %collective-permute-start = (s32[2]{0:T(128)S(1)}, s32[2]{0:T(128)S(1)}, u32[]{:S(2)}, u32[]{:S(2)}) collective-permute-start(s32[2]{0:T(128)S(1)} %get-tuple-element.291), channel_id=1, source_target_pairs={{0,2},{2,4},{4,6},{6,8},{8,10},{10,12},{12,14},{14,16},{16,18},{18... | collective-permute-start | bytes 32 | tf_op jit(solution)/shard_map/ppermute | solution.py:12
  21.5 1.7 %fusion.12 = (f32[2,128,1,128]{3,2,1,0:T(1,128)S(1)}, f32[2,128,1,128]{3,2,1,0:T(1,128)S(1)}) fusion(f32[4,128,32,128]{3,2,1,0:T(8,128)} %copy-done.1), kind=kLoop, calls=%fused_computation.47 | loop fusion | bytes 524288 | tf_op jit(solution)/shard_map/slice | solution.py:63
  23.2 3.4 %collective-permute-start.1 = (f32[2,128,128]{2,1,0:T(8,128)S(1)}, f32[2,128,128]{2,1,0:T(8,128)S(1)}, u32[]{:S(2)}, u32[]{:S(2)}) collective-permute-start(f32[2,128,128]{2,1,0:T(8,128)S(1)} %bitcast.83), channel_id=1, source_target_pairs={{0,2},{2,4},{4,6},{6,8},{8,10},{10,12},{12,14},{14,16},{16,18},{18... | collective-permute-start | bytes 393224 | tf_op jit(solution)/shard_map/ppermute | solution.py:12
  26.6 1.3 collective-permute-start.2
  27.9 1.3 collective-permute-start.3
  32.8 1.2 bitcast_dynamic-update-slice_fusion
  34.0 17.9 %all-reduce.3 = (s32[32]{0:T(128)S(1)}, s32[16]{0:T(128)S(1)}) all-reduce(s32[32]{0:T(128)S(1)} %pad_dynamic-update-slice_fusion, s32[16]{0:T(128)S(1)} %bitcast_dynamic-update-slice_fusion), channel_id=2, replica_groups=mesh['date'=16,'prod'=2] {'date'}, use_global_device_ids=true, to_apply=%add.1 | all-reduce | flops 48 | bytes 384
  53.1 21.4 %all-gather.9.cloned.1.call-done = f32[16,128,1,128]{3,1,2,0:T(8,128)} async-done(((f32[1,128,1,128]{3,1,2,0:T(8,128)}), f32[16,128,1,128]{3,1,2,0:T(8,128)}) %all-gather.9.cloned.1.call-update) | async-done | bytes 1048592 | tf_op jit(solution)/shard_map/all_gather | solution.py:17
  74.6 1.3 reverse_bitcast_fusion
  75.9 28.2 %while.33 = (s32[]{:T(128)}, s32[1]{0:T(128)}, f32[1,128,128]{2,1,0:T(8,128)S(1)}, s32[]{:T(128)}, s32[16,1]{0,1:T(1,128)S(1)}, /*index=5*/f32[16,1,128,128]{3,2,1,0:T(8,128)S(1)}, s32[]{:T(128)}, s32[]{:T(128)}) while((s32[]{:T(128)}, s32[1]{0:T(128)}, f32[1,128,128]{2,1,0:T(8,128)S(1)}, s32[]{:T(128)}, s32[16,1]{0,1:T(1,128)S(1)}, ...), condition=%wide.region_3.4_spmd.clone, body=%wide.region_2.3_spmd.clone.sunk | while | flops 65543 | bytes 196764 | solution.py:29
  105.7 31.4 %all-gather.7.cloned.1.call-done = f32[32,128,128]{2,1,0:T(8,128)} async-done(((f32[2,128,128]{2,1,0:T(8,128)}), f32[32,128,128]{2,1,0:T(8,128)}) %all-gather.7.cloned.1.call-update) | async-done | bytes 2097168 | tf_op jit(solution)/shard_map/all_gather | solution.py:17
  137.1 15.9 %while.32 = (s32[]{:T(128)}, s32[2]{0:T(128)S(1)}, f32[2,128,128]{2,1,0:T(8,128)S(1)}, s32[]{:T(128)}, s32[16,2]{1,0:T(8,128)S(1)}, /*index=5*/f32[16,2,128,128]{3,2,1,0:T(8,128)}, s32[]{:T(128)}, s32[]{:T(128)}) while((s32[]{:T(128)}, s32[2]{0:T(128)S(1)}, f32[2,128,128]{2,1,0:T(8,128)S(1)}, s32[]{:T(128)}, ...), condition=%wide.region_1.2_spmd.clone, body=%wide.region_0.1_spmd.clone.sunk | while | flops 131086 | bytes 393380 | solution.py:29
  143.5 1.0 fusion.18
  144.6 1.0 fusion.18
  145.6 1.0 fusion.18
  146.7 1.0 fusion.18
  147.8 1.0 fusion.18
  148.8 1.0 fusion.18
  153.8 3.2 %fusion.8 = (f32[32,128]{1,0:T(8,128)S(1)}, f32[128,32,128]{2,1,0:T(8,128)}) fusion(f32[128,128]{1,0:T(8,128)S(1)} %get-tuple-element.332, f32[4,128,32,128]{3,2,1,0:T(8,128)} %copy-done.1), kind=kLoop, calls=%fused_computation.45 | loop fusion | flops 1044480 | bytes 4276224 | tf_op jit(solution)/shard_map/reduce_sum | solution.py:87
  157.0 3.6 %fusion.10 = (f32[3,32,128]{2,1,0:T(8,128)S(1)}, f32[3,128,32,128]{3,2,1,0:T(8,128)S(1)}) fusion(f32[3,32]{1,0:T(4,128)S(1)} %get-tuple-element.334, f32[3,128,128]{2,1,0:T(8,128)S(1)} %pad_maximum_fusion.1, f32[3,32]{1,0:T(4,128)S(1)} %get-tuple-element.333, f32[3,128,128]{2,1,0:T(8,128)S(1)} %pad_maximum_fusion, f32[4,128,32,128]{3,2,1,0:T(8,128)} %copy-done.1), kind=kLoop, calls=%fused_computation.46 | loop fusion | flops 7852032 | bytes 13026048 | tf_op jit(solution)/shard_map/reduce_sum | solution.py:87
  160.6 1.9 %all-gather.3 = f32[8,32,128]{2,1,0:T(8,128)S(1)} all-gather(f32[4,32,128]{2,1,0:T(8,128)S(1)} %pad_maximum_fusion.3), channel_id=5, replica_groups=mesh['date'=16,'prod'=2] {'prod'}, dimensions={0}, use_global_device_ids=true | all-gather | bytes 196608 | tf_op jit(solution)/shard_map/all_gather | solution.py:91
  162.5 2.9 %slice_bitcast_fusion = (f32[128,32,128]{2,1,0:T(8,128)}, f32[128,32,128]{2,1,0:T(8,128)}, f32[128,32,128]{2,1,0:T(8,128)}) fusion(f32[3,128,32,128]{3,2,1,0:T(8,128)S(1)} %get-tuple-element.322), kind=kLoop, calls=%fused_computation.12 | loop fusion | bytes 12582912 | tf_op jit(solution)/shard_map/squeeze | solution.py:95
  (119 shorter events, 27.5 us)
Async XLA Ops:
  7.2 1.7 copy-start
  7.2 23.6 %copy-start.5 = (u32[32]{0:T(128)S(1)}, u32[32]{0:T(128)}, u32[]{:S(2)}) copy-start(u32[32]{0:T(128)} %constant.81) | copy-start | bytes 388
  7.2 9.2 %copy-start.4 = (s32[32]{0:T(128)S(1)}, s32[32]{0:T(128)}, u32[]{:S(2)}) copy-start(s32[32]{0:T(128)} %param.9) | copy-start | bytes 388
  7.2 9.2 %copy-start.3 = (s32[32]{0:T(128)S(1)}, s32[32]{0:T(128)}, u32[]{:S(2)}) copy-start(s32[32]{0:T(128)} %param.10) | copy-start | bytes 388
  7.2 22.7 %copy-start.2 = (s32[32]{0:T(128)S(1)}, s32[32]{0:T(128)}, u32[]{:S(2)}) copy-start(s32[32]{0:T(128)} %param.11) | copy-start | bytes 388
  7.2 67.3 %all-gather.9.cloned.1.call-start = ((), (), s32[]{:S(2)}) async-start(), calls=%async_computation.1 | async-start | bytes 1114112 | tf_op jit(solution)/shard_map/all_gather | solution.py:17
  12.3 3.2 %copy-start.1 = (f32[4,128,32,128]{3,2,1,0:T(8,128)}, f32[4,128,32,128]{3,2,1,0:T(8,128)S(1)}, u32[]{:S(2)}) copy-start(f32[4,128,32,128]{3,2,1,0:T(8,128)S(1)} %convolution_bitcast_fusion) | copy-start | bytes 25165828
  16.3 120.8 %all-gather.7.cloned.1.call-start = ((), (), s32[]{:S(2)}) async-start(), calls=%async_computation | async-start | bytes 2228224 | tf_op jit(solution)/shard_map/all_gather | solution.py:17
  16.6 35.6 %collective-permute-start = (s32[2]{0:T(128)S(1)}, s32[2]{0:T(128)S(1)}, u32[]{:S(2)}, u32[]{:S(2)}) collective-permute-start(s32[2]{0:T(128)S(1)} %get-tuple-element.291), channel_id=1, source_target_pairs={{0,2},{2,4},{4,6},{6,8},{8,10},{10,12},{12,14},{14,16},{16,18},{18... | collective-permute-start | bytes 32 | tf_op jit(solution)/shard_map/ppermute | solution.py:12
  23.2 29.1 %collective-permute-start.1 = (f32[2,128,128]{2,1,0:T(8,128)S(1)}, f32[2,128,128]{2,1,0:T(8,128)S(1)}, u32[]{:S(2)}, u32[]{:S(2)}) collective-permute-start(f32[2,128,128]{2,1,0:T(8,128)S(1)} %bitcast.83), channel_id=1, source_target_pairs={{0,2},{2,4},{4,6},{6,8},{8,10},{10,12},{12,14},{14,16},{16,18},{18... | collective-permute-start | bytes 393224 | tf_op jit(solution)/shard_map/ppermute | solution.py:12
  26.6 25.6 %collective-permute-start.2 = (s32[2]{0:T(128)S(1)}, s32[2]{0:T(128)S(1)}, u32[]{:S(2)}, u32[]{:S(2)}) collective-permute-start(s32[2]{0:T(128)S(1)} %get-tuple-element.292), channel_id=1, source_target_pairs={{2,0},{4,2},{6,4},{8,6},{10,8},{12,10},{14,12},{16,14},{18,16},{20... | collective-permute-start | bytes 32 | tf_op jit(solution)/shard_map/ppermute | solution.py:12
  27.9 24.4 %collective-permute-start.3 = (f32[2,128,128]{2,1,0:T(8,128)S(1)}, f32[2,128,128]{2,1,0:T(8,128)S(1)}, u32[]{:S(2)}, u32[]{:S(2)}) collective-permute-start(f32[2,128,128]{2,1,0:T(8,128)S(1)} %bitcast.82), channel_id=1, source_target_pairs={{2,0},{4,2},{6,4},{8,6},{10,8},{12,10},{14,12},{16,14},{18,16},{20... | collective-permute-start | bytes 393224 | tf_op jit(solution)/shard_map/ppermute | solution.py:12
Sparse Core Ops, SparseCore 0:
  16.5 58.0 all-gather.8
  77.9 59.1 all-gather.6
